TPU v7x, 32 devices: a whole 2x2x4 slice. The times are simulated.
32 devices in a mesh: bond: 8 (over z, x), row: 4 (over y, core).
Axes of the slice: x: 2, y: 2, z: 4, core: 2. Of those that a mesh axis runs over, the one named last changes fastest.
Arguments:
- left_site: bfloat16 [16384, 1024], P(('bond', 'row')), may hold values from -6 to 6
- right_site: bfloat16 [8192, 2048], P(('bond', 'row')), may hold values from -0.1875 to 0.1875
- gate: float32 [4, 4], replicated, may hold values from -3 to 3
- omega: bfloat16 [2048, 1024], P(('bond', 'row')), may hold values from -0.125 to 0.125
Outputs:
- left_new: bfloat16 [16384, 1024], P(('bond', 'row'))
- right_new: bfloat16 [8192, 2048], P(('bond', 'row'))
- odd_pair: bfloat16 [16384, 2048], P(('bond', 'row'))
All inputs are finite; a program needn't handle non-finite values.
Results may differ from a plain program's by a relative error of at most 0.03.
Values may be sent and summed in bfloat16 or wider, within the bound.
A program may use at most 128 MiB of HBM per device.

v0:
```python
import math

import jax
import jax.numpy as jnp
from jax import lax
from jax.sharding import PartitionSpec as P


def from_behind(block, axis, distance):
    devices = range(lax.axis_size(axis))
    route = [(i - distance, i) for i in devices if i - distance in devices]
    return lax.ppermute(block, axis, route)


def shards(left_site, right_site, gate, omega):
    row_count = left_site.shape[0]
    bond_width = left_site.shape[1]
    kept_rank = omega.shape[1]
    columns = left_site
    product = jnp.dot(
        columns,
        lax.all_gather(right_site, "row", axis=0, tiled=True),
        preferred_element_type=jnp.float32,
    )
    mixed = jnp.einsum(
        "stuv,auvc->astc",
        gate.reshape(2, 2, 2, 2),
        product.reshape(row_count // 2, 2, 2, bond_width),
    )
    theta = mixed.reshape(row_count, 2 * bond_width).astype(jnp.bfloat16)
    columns = theta
    sketch = jnp.dot(
        columns,
        lax.all_gather(omega, ("bond", "row"), axis=0, tiled=True),
        preferred_element_type=jnp.float32,
    )
    local_gram = jnp.dot(sketch.T, sketch, precision=lax.Precision.HIGHEST)
    gram = lax.psum(local_gram, "row") / (2.0 * bond_width)
    diag_mean = jnp.trace(gram) / kept_rank
    lower = jnp.linalg.cholesky(gram + 0.01 * diag_mean * jnp.eye(kept_rank, dtype=jnp.float32))
    basis = lax.linalg.triangular_solve(
        lower, sketch, left_side=False, lower=True, transpose_a=True
    )
    left_new = basis.astype(jnp.bfloat16)
    right_scale = 1.0 / math.sqrt(2.0 * bond_width)
    own_rows = kept_rank // lax.axis_size("row")
    columns = left_new
    right_new = lax.psum_scatter(
        (
            lax.dot_general(
                columns, theta, (((0,), (0,)), ((), ())), preferred_element_type=jnp.float32
            )
            * right_scale
        ).astype(jnp.bfloat16),
        "row",
        scatter_dimension=0,
        tiled=True,
    )
    following = from_behind(left_new.reshape(row_count // 2, 2 * kept_rank), "bond", -1)
    right_view = right_new.reshape(2 * own_rows, bond_width)
    columns = right_view
    pair_sum = jnp.dot(
        columns,
        lax.all_gather(following, "row", axis=0, tiled=True),
        preferred_element_type=jnp.float32,
    )
    odd_pair = (pair_sum * (1.0 / math.sqrt(1.0 * bond_width))).astype(jnp.bfloat16)
    return (left_new, right_new, odd_pair)


def solution(mesh):
    placed = (P(("bond", "row"), None), P(("bond", "row"), None), P(), P(("bond", "row"), None))
    return jax.shard_map(
        shards,
        mesh=mesh,
        in_specs=placed,
        out_specs=(P(("bond", "row"), None), P(("bond", "row"), None), P(("bond", "row"), None)),
        check_vma=False,
    )
```

profile of v0, /device:TPU:0, one launch (start us, length us, event | category | flops | bytes accessed | tf_op | source)
XLA Modules:
  0.0 673.8 jit_solution(335509559467034745)
XLA Ops:
  9.5 37.3 %all-gather.4.cloned.1.call-done = bf16[1024,2048]{1,0:T(8,128)(2,1)} async-done(((bf16[256,2048]{1,0:T(8,128)(2,1)}), bf16[1024,2048]{1,0:T(8,128)(2,1)}) %all-gather.4.cloned.1.call-update) | async-done | bytes 4194320 | tf_op jit(solution)/shard_map/all_gather | solution.py:22
  61.5 49.8 %all-gather.6.cloned.1.call-done = bf16[2048,1024]{1,0:T(8,128)(2,1)} async-done(((bf16[64,1024]{1,0:T(8,128)(2,1)}), bf16[2048,1024]{1,0:T(8,128)(2,1)}) %all-gather.6.cloned.1.call-update) | async-done | bytes 4194320 | tf_op jit(solution)/shard_map/all_gather | solution.py:34
  116.4 8.4 %fusion.70 = f32[1024,1024]{0,1:T(8,128)} fusion(f32[512,1024]{1,0:T(8,128)S(1)} %fusion.69), kind=kOutput, calls=%fused_computation.167 | convolution fusion | flops 6442450944 | bytes 6291456 | tf_op jit(solution)/shard_map/dot_general | solution.py:37
  125.0 84.3 %all-reduce.3.cloned.1.call-done = f32[1024,1024]{0,1:T(8,128)} async-done(((f32[1024,1024]{0,1:T(8,128)}), f32[1024,1024]{0,1:T(8,128)}) %all-reduce.3.cloned.1.call-update) | async-done | bytes 4194320 | tf_op jit(solution)/shard_map/psum | solution.py:38
  229.8 11.7 %cholesky.222 = f32[128,128]{1,0:T(8,128)S(1)} custom-call(f32[128,128]{1,0:T(8,128)S(1)} %cholesky.577), custom_call_target="Cholesky" | custom-call | tf_op jit(solution)/shard_map/jit(cholesky)/cholesky | solution.py:40
  241.7 9.8 %custom-call.62 = f32[1,128,128]{1,2,0:T(8,128)S(1)} custom-call(f32[1,128,128]{2,1,0:T(8,128)S(1)} %get-tuple-element.73), custom_call_target="InvertDiagBlocksLowerTriangular" | custom-call | tf_op jit(solution)/shard_map/jit(cholesky)/cholesky | solution.py:40
  254.8 11.7 %cholesky.243 = f32[128,128]{1,0:T(8,128)S(1)} custom-call(f32[128,128]{1,0:T(8,128)S(1)} %cholesky.581), custom_call_target="Cholesky" | custom-call | tf_op jit(solution)/shard_map/jit(cholesky)/cholesky | solution.py:40
  267.0 9.8 %custom-call.63 = f32[1,128,128]{1,2,0:T(8,128)S(1)} custom-call(f32[1,128,128]{2,1,0:T(8,128)S(1)} %get-tuple-element.71), custom_call_target="InvertDiagBlocksLowerTriangular" | custom-call | tf_op jit(solution)/shard_map/jit(cholesky)/cholesky | solution.py:40
  282.4 11.7 %cholesky.466 = f32[128,128]{1,0:T(8,128)S(1)} custom-call(f32[128,128]{1,0:T(8,128)S(1)} %cholesky.586), custom_call_target="Cholesky" | custom-call | tf_op jit(solution)/shard_map/jit(cholesky)/cholesky | solution.py:40
  294.9 9.8 %custom-call.64 = f32[1,128,128]{1,2,0:T(8,128)S(1)} custom-call(f32[1,128,128]{2,1,0:T(8,128)S(1)} %get-tuple-element.69), custom_call_target="InvertDiagBlocksLowerTriangular" | custom-call | tf_op jit(solution)/shard_map/jit(cholesky)/cholesky | solution.py:40
  309.3 11.7 %cholesky.485 = f32[128,128]{1,0:T(8,128)S(1)} custom-call(f32[128,128]{1,0:T(8,128)S(1)} %cholesky.591), custom_call_target="Cholesky" | custom-call | tf_op jit(solution)/shard_map/jit(cholesky)/cholesky | solution.py:40
  321.7 9.8 %custom-call.65 = f32[1,128,128]{1,2,0:T(8,128)S(1)} custom-call(f32[1,128,128]{2,1,0:T(8,128)S(1)} %get-tuple-element.67), custom_call_target="InvertDiagBlocksLowerTriangular" | custom-call | tf_op jit(solution)/shard_map/jit(cholesky)/cholesky | solution.py:40
  335.9 12.1 %cholesky.504 = f32[128,128]{1,0:T(8,128)S(1)} custom-call(f32[128,128]{1,0:T(8,128)S(1)} %cholesky.596), custom_call_target="Cholesky" | custom-call | tf_op jit(solution)/shard_map/jit(cholesky)/cholesky | solution.py:40
  348.7 9.8 %custom-call.66 = f32[1,128,128]{1,2,0:T(8,128)S(1)} custom-call(f32[1,128,128]{2,1,0:T(8,128)S(1)} %get-tuple-element.65), custom_call_target="InvertDiagBlocksLowerTriangular" | custom-call | tf_op jit(solution)/shard_map/jit(cholesky)/cholesky | solution.py:40
  362.8 11.7 %cholesky.524 = f32[128,128]{1,0:T(8,128)S(1)} custom-call(f32[128,128]{1,0:T(8,128)S(1)} %cholesky.601), custom_call_target="Cholesky" | custom-call | tf_op jit(solution)/shard_map/jit(cholesky)/cholesky | solution.py:40
  375.2 9.8 %custom-call.67 = f32[1,128,128]{1,2,0:T(8,128)S(1)} custom-call(f32[1,128,128]{2,1,0:T(8,128)S(1)} %get-tuple-element.63), custom_call_target="InvertDiagBlocksLowerTriangular" | custom-call | tf_op jit(solution)/shard_map/jit(cholesky)/cholesky | solution.py:40
  388.9 11.7 %cholesky.544 = f32[128,128]{1,0:T(8,128)S(1)} custom-call(f32[128,128]{1,0:T(8,128)S(1)} %cholesky.606), custom_call_target="Cholesky" | custom-call | tf_op jit(solution)/shard_map/jit(cholesky)/cholesky | solution.py:40
  401.4 9.8 %custom-call.68 = f32[1,128,128]{1,2,0:T(8,128)S(1)} custom-call(f32[1,128,128]{2,1,0:T(8,128)S(1)} %get-tuple-element.61), custom_call_target="InvertDiagBlocksLowerTriangular" | custom-call | tf_op jit(solution)/shard_map/jit(cholesky)/cholesky | solution.py:40
  414.2 11.7 %cholesky.562 = f32[128,128]{1,0:T(8,128)S(1)} custom-call(f32[128,128]{1,0:T(8,128)S(1)} %convolution_subtract_fusion.13), custom_call_target="Cholesky" | custom-call | tf_op jit(solution)/shard_map/jit(cholesky)/cholesky | solution.py:40
  441.3 28.6 %while.1 = (s32[]{:T(128)}, f32[1024,1024]{0,1:T(8,128)}, s32[8,2]{0,1:T(2,128)S(1)}, f32[8,128,128]{2,1,0:T(8,128)}, s32[]{:T(128)}) while((s32[]{:T(128)}, f32[1024,1024]{0,1:T(8,128)}, s32[8,2]{0,1:T(2,128)S(1)}, f32[8,128,128]{2,1,0:T(8,128)}, s32[]{:T(128)}) %tuple.57), condition=%wide.while_cond, body=%wide.while_body.sunk | while | flops 2 | bytes 393329 | solution.py:41
  469.9 80.2 %custom-call.69 = f32[8,128,128]{1,2,0:T(8,128)} custom-call(f32[8,128,128]{2,1,0:T(8,128)} %get-tuple-element.10), custom_call_target="InvertDiagBlocksLowerTriangular" | custom-call | tf_op jit(solution)/shard_map/triangular_solve | solution.py:41
  582.0 25.2 %collective-permute-done = bf16[256,2048]{1,0:T(8,128)(2,1)S(1)} collective-permute-done((bf16[256,2048]{1,0:T(8,128)(2,1)S(1)}, bf16[256,2048]{1,0:T(8,128)(2,1)S(1)}, u32[]{:S(2)}, u32[]{:S(2)}) %collective-permute-start) | collective-permute-done | bytes 1048608 | tf_op jit(solution)/shard_map/ppermute | solution.py:12
  608.2 16.4 %reduce-scatter.2.cloned.1.call-done = bf16[256,2048]{1,0:T(8,128)(2,1)} async-done(((bf16[1024,2048]{1,0:T(8,128)(2,1)}), bf16[256,2048]{1,0:T(8,128)(2,1)}) %reduce-scatter.2.cloned.1.call-update) | async-done | bytes 1048592 | tf_op jit(solution)/shard_map/reduce_scatter | solution.py:48
  626.0 35.0 %all-gather.8.cloned.1.call-done = bf16[1024,2048]{1,0:T(8,128)(2,1)} async-done(((bf16[256,2048]{1,0:T(8,128)(2,1)}), bf16[1024,2048]{1,0:T(8,128)(2,1)}) %all-gather.8.cloned.1.call-update) | async-done | bytes 4194320 | tf_op jit(solution)/shard_map/all_gather | solution.py:64
  (155 shorter events, 154.0 us)
Async XLA Ops:
  7.2 39.6 %copy-start = (bf16[512,1024]{1,0:T(8,128)(2,1)S(1)}, bf16[512,1024]{1,0:T(8,128)(2,1)}, u32[]{:S(2)}) copy-start(bf16[512,1024]{1,0:T(8,128)(2,1)} %param.4) | copy-start | bytes 3145732
  7.2 39.6 %all-gather.4.cloned.1.call-start = ((), (), s32[]{:S(2)}) async-start(), calls=%async_computation.1 | async-start | bytes 5242880 | tf_op jit(solution)/shard_map/all_gather | solution.py:22
  7.9 103.4 %all-gather.6.cloned.1.call-start = ((), (), s32[]{:S(2)}) async-start(), calls=%async_computation.2 | async-start | bytes 4325376 | tf_op jit(solution)/shard_map/all_gather | solution.py:34
  8.7 200.6 %all-reduce.3.cloned.1.call-start = ((), (), s32[]{:S(2)}) async-start(), calls=%async_computation.3 | async-start | bytes 8388608 | tf_op jit(solution)/shard_map/psum | solution.py:38
  124.9 499.6 %reduce-scatter.2.cloned.1.call-start = ((), (), s32[]{:S(2)}) async-start(), calls=%async_computation.4 | async-start | bytes 5242880 | tf_op jit(solution)/shard_map/reduce_scatter | solution.py:48
  227.9 1.9 copy-start.3
  278.0 2.0 copy-start.2
  550.1 6.0 copy-start.7
  565.9 9.4 %copy-start.5 = (bf16[64,8,2,1024]{3,1,2,0:T(8,128)(2,1)S(1)}, bf16[64,8,2,1024]{3,1,2,0:T(8,128)(2,1)}, u32[]{:S(2)}) copy-start(bf16[64,8,2,1024]{3,1,2,0:T(8,128)(2,1)} %copy.58) | copy-start | bytes 6291460
  579.7 81.3 %all-gather.8.cloned.1.call-start = ((), (), s32[]{:S(2)}) async-start(), calls=%async_computation.5 | async-start | bytes 5242880 | tf_op jit(solution)/shard_map/all_gather | solution.py:64
  580.3 86.6 %copy-start.4 = (bf16[512,1024]{1,0:T(8,128)(2,1)}, bf16[512,1024]{1,0:T(8,128)(2,1)S(1)}, u32[]{:S(2)}) copy-start(bf16[512,1024]{1,0:T(8,128)(2,1)S(1)} %copy.47) | copy-start | bytes 3145732
  580.7 26.5 %collective-permute-start = (bf16[256,2048]{1,0:T(8,128)(2,1)S(1)}, bf16[256,2048]{1,0:T(8,128)(2,1)S(1)}, u32[]{:S(2)}, u32[]{:S(2)}) collective-permute-start(bf16[256,2048]{1,0:T(8,128)(2,1)S(1)} %convert_element_type.28), channel_id=1, source_target_pairs={{4,0},{8,4},{12,8},{16,12},{20,16},{24,20},{28,24},{5,1},{9,5},{13... | collective-permute-start | bytes 3145736 | tf_op jit(solution)/shard_map/ppermute | solution.py:12
  607.2 1.0 copy-start.6
  624.5 42.3 %copy-start.1 = (bf16[512,1024]{1,0:T(8,128)(2,1)S(1)}, bf16[512,1024]{1,0:T(8,128)(2,1)}, u32[]{:S(2)}) copy-start(bf16[512,1024]{1,0:T(8,128)(2,1)} %param.4) | copy-start | bytes 3145732
Sparse Core Ops, SparseCore 0:
  9.5 37.1 all-gather.3
  49.6 61.6 all-gather.5
  125.0 84.2 all-reduce.2
  579.8 44.6 reduce-scatter.1
  626.5 34.4 all-gather.7
where the time goes:
time: 683 us; the launch traced here: 674 us
  other arithmetic  265 us (39%)
  waiting for transfers between devices  249 us (36%)
  matrix products  84.2 us (12%)
  local copies, waits for them, and re-layouts  53.1 us (8%)
  between operations  20.4 us (3%)
    another operation x30, other arithmetic, shards(): jnp.linalg.cholesky(gram + 0.01 * diag_mean * jnp.eye(kept_rank, dtype=jn...  168 us
    another operation x3, other arithmetic, shards(): lax.linalg.triangular_solve(lower, sketch, left_side=False, lower=True, t...  85.1 us
    psum x1, waiting for transfers between devices, shards(): gram = lax.psum(local_gram, 'row') / (2.0 * bond_width)  84.3 us
    all_gather x1, waiting for transfers between devices, shards(): lax.all_gather(omega, ('bond', 'row'), axis=0, tiled=True)  49.8 us
    all_gather x1, waiting for transfers between devices, shards(): lax.all_gather(right_site, 'row', axis=0, tiled=True)  37.3 us
    all_gather x1, waiting for transfers between devices, shards(): lax.all_gather(following, 'row', axis=0, tiled=True)  35 us
    another operation x40, local copies, waits for them, and re-layouts  28.5 us
    another operation x14, matrix products, shards(): jnp.linalg.cholesky(gram + 0.01 * diag_mean * jnp.eye(kept_rank, dtype=jn...  25.9 us
  transfers between devices with their start and end apart: 6, of which 6 were waited for; matrix products, arithmetic and copies ran while one was open for 3% of the time, Pallas kernels for 0%

commit v1 on v0

v1 whole, which is shorter than its diff:
```python
import functools
import math

import jax
import jax.numpy as jnp
from jax import lax
from jax.experimental import pallas as pl
from jax.experimental.pallas import tpu as pltpu
from jax.sharding import PartitionSpec as P

LANES = 128
SUB = 8


def from_behind(block, axis, distance):
    devices = range(lax.axis_size(axis))
    route = [(i - distance, i) for i in devices if i - distance in devices]
    return lax.ppermute(block, axis, route)


def split(x):
    high = x.astype(jnp.bfloat16)
    return high, (x - high.astype(jnp.float32)).astype(jnp.bfloat16)


def inverse_factor(block):
    groups = LANES // SUB
    lane = lax.broadcasted_iota(jnp.int32, (SUB, LANES), 1)
    sub = lax.broadcasted_iota(jnp.int32, (SUB, LANES), 0)
    left = [block[g * SUB:(g + 1) * SUB, :] for g in range(groups)]
    right = [jnp.where(lane == sub + g * SUB, 1.0, 0.0) for g in range(groups)]
    rows = []

    def over_lanes(x, column):
        return jnp.broadcast_to(x[:, column:column + 1], (SUB, LANES))

    def over_rows(x, row):
        return jnp.broadcast_to(x[row:row + 1, :], (SUB, LANES))

    for g in range(groups):
        a, e = left[g], right[g]
        cols = [over_lanes(a, g * SUB + c) for c in range(SUB)]
        finished = jnp.zeros_like(e)
        for k in range(SUB):
            here = sub == k
            pivot = over_rows(cols[k], k)
            inverse = 1.0 / pivot
            factor = cols[k] * inverse
            row_a, row_e = over_rows(a, k), over_rows(e, k)
            finished = jnp.where(here, row_e * lax.rsqrt(pivot), finished)
            a = jnp.where(here, row_a * inverse, a - factor * row_a)
            e = jnp.where(here, row_e * inverse, e - factor * row_e)
            for c in range(k + 1, SUB):
                row_c = over_rows(cols[c], k)
                cols[c] = jnp.where(here, row_c * inverse, cols[c] - factor * row_c)
        rows.append(finished)
        if g + 1 == groups:
            break
        wide_a = [over_rows(a, k) for k in range(SUB)]
        wide_e = [over_rows(e, k) for k in range(SUB)]
        for i in range(g + 1, groups):
            coeff = [over_lanes(left[i], g * SUB + c) for c in range(SUB)]
            for c in range(SUB):
                left[i] = left[i] - coeff[c] * wide_a[c]
                right[i] = right[i] - coeff[c] * wide_e[c]
    return jnp.concatenate(rows, axis=0)


def solve_kernel(scale, gram_ref, sketch_ref, flat_ref, tall_ref, work, wide):
    size = gram_ref.shape[0]
    blocks = size // LANES
    width = size + sketch_ref.shape[1]
    eye = (
        lax.broadcasted_iota(jnp.int32, (LANES, LANES), 0)
        == lax.broadcasted_iota(jnp.int32, (LANES, LANES), 1)
    )

    total = jnp.zeros((LANES, LANES), jnp.float32)
    for d in range(blocks):
        at = slice(d * LANES, (d + 1) * LANES)
        total = total + jnp.where(eye, gram_ref[at, at], 0.0)
    ridge = jnp.sum(total, keepdims=True) * (scale * 0.01 / size)
    for d in range(blocks):
        at = slice(d * LANES, (d + 1) * LANES)
        work[at, :size] = gram_ref[at, :] * scale
        work[at, size:] = sketch_ref[at, :]
        work[at, at] = work[at, at] + jnp.where(eye, ridge, 0.0)

    def eliminate(d, carry):
        start = pl.multiple_of(d * LANES, LANES)
        here = pl.ds(start, LANES)
        inverse = inverse_factor(work[here, here])
        high, low = split(inverse)
        factor = jnp.concatenate([high, high, low], axis=1)
        high, low = split(work[here, :])
        solved = jnp.dot(
            factor,
            jnp.concatenate([high, low, high], axis=0),
            preferred_element_type=jnp.float32,
        )
        work[here, :] = solved
        high, low = split(solved)
        wide[0:LANES, :] = high
        wide[LANES:2 * LANES, :] = low
        wide[2 * LANES:, :] = high
        basis = solved[:, size:]
        flat_ref[here, :] = basis.astype(jnp.bfloat16)
        tall_ref[:, here] = basis.T.astype(jnp.bfloat16)

        def update(i, carry):
            there = pl.ds(pl.multiple_of(i * LANES, LANES), LANES)
            high, low = split(work[here, there].T)
            lower = jnp.concatenate([high, high, low], axis=1)
            work[there, :] = work[there, :] - jnp.dot(
                lower, wide[...], preferred_element_type=jnp.float32
            )
            return carry

        return lax.fori_loop(d + 1, blocks, update, carry)

    lax.fori_loop(0, blocks, eliminate, 0)


def solve(gram, sketch_t, scale):
    size, rows = sketch_t.shape
    return pl.pallas_call(
        functools.partial(solve_kernel, scale),
        out_shape=(
            jax.ShapeDtypeStruct((size, rows), jnp.bfloat16),
            jax.ShapeDtypeStruct((rows, size), jnp.bfloat16),
        ),
        in_specs=[pl.BlockSpec(memory_space=pltpu.VMEM)] * 2,
        out_specs=(pl.BlockSpec(memory_space=pltpu.VMEM),) * 2,
        scratch_shapes=[
            pltpu.VMEM((size, size + rows), jnp.float32),
            pltpu.VMEM((3 * LANES, size + rows), jnp.bfloat16),
        ],
        compiler_params=pltpu.CompilerParams(vmem_limit_bytes=48 * 1024 * 1024),
        cost_estimate=pl.CostEstimate(
            flops=4 * size * size * (size + rows), bytes_accessed=4 * size * (size + 2 * rows), transcendentals=size
        ),
        name="solve",
    )(gram, sketch_t)


def shards(left_site, right_site, gate, omega):
    row_count = left_site.shape[0]
    bond_width = left_site.shape[1]
    kept_rank = omega.shape[1]
    product = jnp.dot(
        left_site,
        lax.all_gather(right_site, "row", axis=0, tiled=True),
        preferred_element_type=jnp.float32,
    )
    mixed = jnp.einsum(
        "stuv,auvc->astc",
        gate.reshape(2, 2, 2, 2),
        product.reshape(row_count // 2, 2, 2, bond_width),
    )
    theta = mixed.reshape(row_count, 2 * bond_width).astype(jnp.bfloat16)
    sketch_t = lax.dot_general(
        lax.all_gather(omega, ("bond", "row"), axis=0, tiled=True),
        theta,
        (((0,), (1,)), ((), ())),
        preferred_element_type=jnp.float32,
    )
    high, low = split(sketch_t)
    over = (((1,), (1,)), ((), ()))
    local_gram = lax.dot_general(
        jnp.concatenate([high, high, low], axis=1),
        jnp.concatenate([high, low, high], axis=1),
        over,
        preferred_element_type=jnp.float32,
    )
    gram = lax.psum(local_gram, "row")
    left_t, left_new = solve(gram, sketch_t, 1.0 / (2.0 * bond_width))
    right_scale = 1.0 / math.sqrt(2.0 * bond_width)
    own_rows = kept_rank // lax.axis_size("row")
    following = from_behind(left_new.reshape(row_count // 2, 2 * kept_rank), "bond", -1)
    right_new = lax.psum_scatter(
        (jnp.dot(left_t, theta, preferred_element_type=jnp.float32) * right_scale).astype(jnp.bfloat16),
        "row",
        scatter_dimension=0,
        tiled=True,
    )
    right_view = right_new.reshape(2 * own_rows, bond_width)
    pair_sum = jnp.dot(
        right_view,
        lax.all_gather(following, "row", axis=0, tiled=True),
        preferred_element_type=jnp.float32,
    )
    odd_pair = (pair_sum * (1.0 / math.sqrt(1.0 * bond_width))).astype(jnp.bfloat16)
    return (left_new, right_new, odd_pair)


def solution(mesh):
    placed = (P(("bond", "row"), None), P(("bond", "row"), None), P(), P(("bond", "row"), None))
    return jax.shard_map(
        shards,
        mesh=mesh,
        in_specs=placed,
        out_specs=(P(("bond", "row"), None), P(("bond", "row"), None), P(("bond", "row"), None)),
        check_vma=False,
    )
```

time: 683 us -> 361 us (0.53); the launches traced: 674 us -> 360 us
  other arithmetic: 265 us -> 0 us
  Pallas kernels: 0 us -> 56 us
  matrix products: 84.2 us -> 30.3 us
  local copies, waits for them, and re-layouts: 53.1 us -> 9.91 us
    another operation x33 -> x0, other arithmetic: 253 us -> none  [the longest x30 168 us: shards(): jnp.linalg.cholesky(gram + 0.01 * diag_mean * jnp.eye(kept_rank, dtype=jn...]
    pallas_call x0 -> x1, Pallas kernels: none -> 56 us  [solve(): pl.pallas_call(functools.partial(solve_kernel, scale), out_shape=(jax.Sha...]
    another operation x29 -> x0, matrix products: 51 us -> none  [the longest x14 25.9 us: shards(): jnp.linalg.cholesky(gram + 0.01 * diag_mean * jnp.eye(kept_rank, dtype=jn...]
    another operation x66 -> x0, local copies, waits for them, and re-layouts: 34.3 us -> none
  transfers between devices with their start and end apart: 6 -> 6, of which waited for: 6 -> 6; matrix products, arithmetic and copies ran while one was open for 3% -> 5% of each run, Pallas kernels for 0% -> 0%
where the time goes in v1:
time: 361 us; the launch traced here: 360 us
  waiting for transfers between devices  249 us (69%)
  Pallas kernels  56 us (16%)
  matrix products  30.3 us (8%)
  between operations  13.8 us (4%)
  local copies, waits for them, and re-layouts  9.91 us (3%)
    psum x1, waiting for transfers between devices, shards(): gram = lax.psum(local_gram, 'row')  84.2 us
    pallas_call x1, Pallas kernels, solve(): pl.pallas_call(functools.partial(solve_kernel, scale), out_shape=(jax.Sha...  56 us
    all_gather x1, waiting for transfers between devices, shards(): lax.all_gather(omega, ('bond', 'row'), axis=0, tiled=True)  49.7 us
    all_gather x1, waiting for transfers between devices, shards(): lax.all_gather(right_site, 'row', axis=0, tiled=True)  37.3 us
    all_gather x1, waiting for transfers between devices, shards(): lax.all_gather(following, 'row', axis=0, tiled=True)  35 us
    ppermute x1, waiting for transfers between devices, from_behind(): return lax.ppermute(block, axis, route)  25.2 us
    reduce_scatter x1, waiting for transfers between devices, shards(): lax.psum_scatter((jnp.dot(left_t, theta, preferred_element_type=jnp.float...  15.8 us
  transfers between devices with their start and end apart: 6, of which 6 were waited for; matrix products, arithmetic and copies ran while one was open for 5% of the time, Pallas kernels for 0%

profile of v1, /device:TPU:0, one launch (start us, length us, event | category | flops | bytes accessed | tf_op | source)
XLA Modules:
  0.0 360.4 jit_solution(15378613777276414053)
XLA Ops:
  7.2 0.7 all-gather.4.cloned.1.call-update
  8.0 0.7 all-gather.6.cloned.1.call-update
  8.7 0.8 reshape.21
  9.5 37.3 %all-gather.4.cloned.1.call-done = bf16[1024,2048]{1,0:T(8,128)(2,1)} async-done(((bf16[256,2048]{1,0:T(8,128)(2,1)}), bf16[1024,2048]{1,0:T(8,128)(2,1)}) %all-gather.4.cloned.1.call-update) | async-done | bytes 4194320 | tf_op jit(solution)/shard_map/all_gather | solution.py:152
  46.8 5.8 %fusion.16 = bf16[512,2048]{1,0:T(8,128)(2,1)} fusion(bf16[512,1024]{1,0:T(8,128)(2,1)S(1)} %copy-done, bf16[1024,2048]{1,0:T(8,128)(2,1)} %all-gather.4.cloned.1.call-done), kind=kOutput, calls=%fused_computation.19 | convolution fusion | flops 2147483648 | bytes 7340032 | tf_op jit(solution)/shard_map/dot_general | solution.py:150
  52.6 3.3 reshape.24
  55.9 3.7 %bitcast_convert_fusion = bf16[256,1024,2,2]{1,3,2,0:T(2,128)(2,1)S(1)} fusion(bf16[256,2,2,1024,1]{3,2,1,0,4:T(2,128)(2,1)S(1)} %reshape.24, bf16[2,2,2,2]{3,2,1,0:T(2,128)(2,1)S(1)} %reshape.21), kind=kOutput, calls=%fused_computation.1 | convolution fusion | flops 8388608 | bytes 4194336 | tf_op jit(solution)/shard_map/stuv,auvc->astc/dot_general | solution.py:155
  59.6 1.9 copy.12
  61.5 49.7 %all-gather.6.cloned.1.call-done = bf16[2048,1024]{1,0:T(8,128)(2,1)} async-done(((bf16[64,1024]{1,0:T(8,128)(2,1)}), bf16[2048,1024]{1,0:T(8,128)(2,1)}) %all-gather.6.cloned.1.call-update) | async-done | bytes 4194320 | tf_op jit(solution)/shard_map/all_gather | solution.py:162
  111.3 5.2 %subtract_convert_fusion = (bf16[1024,512]{1,0:T(8,128)(2,1)S(1)}, bf16[1024,512]{1,0:T(8,128)(2,1)S(1)}, f32[1024,512]{1,0:T(8,128)S(1)}) fusion(bf16[512,2048]{1,0:T(8,128)(2,1)} %bitcast.25, bf16[2048,1024]{1,0:T(8,128)(2,1)} %all-gather.6.cloned.1.call-done), kind=kOutput, calls=%fused_computation.14 | convolution fusion | flops 2149580800 | bytes 10485760 | tf_op jit(solution)/shard_map/dot_general | solution.py:161
  116.5 5.4 %fusion.5 = f32[1024,1024]{1,0:T(8,128)} fusion(bf16[1024,512]{1,0:T(8,128)(2,1)S(1)} %get-tuple-element.8, bf16[1024,512]{1,0:T(8,128)(2,1)S(1)} %get-tuple-element.7), kind=kOutput, calls=%fused_computation.8 | convolution fusion | flops 3240099840 | bytes 6291456 | tf_op jit(solution)/shard_map/dot_general | solution.py:169
  121.9 0.2 reduce-scatter.2.cloned.1.call-start
  122.2 84.2 %all-reduce.2.cloned.1.call-done.gram_ref = f32[1024,1024]{1,0:T(8,128)} async-done(((f32[1024,1024]{1,0:T(8,128)}), f32[1024,1024]{1,0:T(8,128)}) %all-reduce.2.cloned.1.call-update) | async-done | bytes 4194320 | tf_op jit(solution)/shard_map/psum | solution.py:175
  206.4 56.0 %solve.1 = (bf16[1024,512]{1,0:T(8,128)(2,1)S(1)}, bf16[512,1024]{1,0:T(8,128)(2,1)}) custom-call(f32[1024,1024]{1,0:T(8,128)} %all-reduce.2.cloned.1.call-done.gram_ref, f32[1024,512]{1,0:T(8,128)S(1)} %get-tuple-element.9.sketch_ref), custom_call_target="tpu_custom_call" | custom-call | flops 6442450944 | bytes 8388608 | tf_op jit(solution)/shard_map/solve/pallas_call | solution.py:126
  262.3 4.3 %multiply_convert_fusion = bf16[1024,2048]{1,0:T(8,128)(2,1)} fusion(bf16[1024,512]{1,0:T(8,128)(2,1)S(1)} %get-tuple-element.6, bf16[512,2048]{1,0:T(8,128)(2,1)S(1)} %bitcast.26), kind=kOutput, calls=%fused_computation | convolution fusion | flops 2151677952 | bytes 7340032 | tf_op jit(solution)/shard_map/dot_general | solution.py:181
  266.7 1.1 copy-done.2
  267.9 0.4 reshape.23
  268.3 1.3 collective-permute-start
  269.6 25.2 %collective-permute-done = bf16[256,2048]{1,0:T(8,128)(2,1)S(1)} collective-permute-done((bf16[256,2048]{1,0:T(8,128)(2,1)S(1)}, bf16[256,2048]{1,0:T(8,128)(2,1)S(1)}, u32[]{:S(2)}, u32[]{:S(2)}) %collective-permute-start) | collective-permute-done | bytes 1048608 | tf_op jit(solution)/shard_map/ppermute | solution.py:18
  294.7 1.0 copy-done.3
  295.7 15.8 %reduce-scatter.2.cloned.1.call-done = bf16[256,2048]{1,0:T(8,128)(2,1)} async-done(((bf16[1024,2048]{1,0:T(8,128)(2,1)}), bf16[256,2048]{1,0:T(8,128)(2,1)}) %reduce-scatter.2.cloned.1.call-update) | async-done | bytes 1048592 | tf_op jit(solution)/shard_map/reduce_scatter | solution.py:180
  311.6 1.4 reshape.22
  313.0 35.0 %all-gather.8.cloned.1.call-done = bf16[1024,2048]{1,0:T(8,128)(2,1)} async-done(((bf16[256,2048]{1,0:T(8,128)(2,1)}), bf16[1024,2048]{1,0:T(8,128)(2,1)}) %all-gather.8.cloned.1.call-update) | async-done | bytes 4194320 | tf_op jit(solution)/shard_map/all_gather | solution.py:189
  348.0 5.8 %multiply_convert_fusion.1 = bf16[512,2048]{1,0:T(8,128)(2,1)} fusion(bf16[512,1024]{1,0:T(8,128)(2,1)S(1)} %reshape.22, bf16[1024,2048]{1,0:T(8,128)(2,1)} %all-gather.8.cloned.1.call-done), kind=kOutput, calls=%fused_computation.4 | convolution fusion | flops 2149580800 | bytes 7340032 | tf_op jit(solution)/shard_map/dot_general | solution.py:187
  (13 shorter events, 0.2 us)
Async XLA Ops:
  7.2 39.6 %copy-start = (bf16[512,1024]{1,0:T(8,128)(2,1)S(1)}, bf16[512,1024]{1,0:T(8,128)(2,1)}, u32[]{:S(2)}) copy-start(bf16[512,1024]{1,0:T(8,128)(2,1)} %param.4) | copy-start | bytes 3145732
  7.2 39.6 %all-gather.4.cloned.1.call-start = ((), (), s32[]{:S(2)}) async-start(), calls=%async_computation.1 | async-start | bytes 5242880 | tf_op jit(solution)/shard_map/all_gather | solution.py:152
  7.9 103.4 %all-gather.6.cloned.1.call-start = ((), (), s32[]{:S(2)}) async-start(), calls=%async_computation.2 | async-start | bytes 4325376 | tf_op jit(solution)/shard_map/all_gather | solution.py:162
  8.7 197.7 %all-reduce.2.cloned.1.call-start = ((), (), s32[]{:S(2)}) async-start(), calls=%async_computation.3 | async-start | bytes 8388608 | tf_op jit(solution)/shard_map/psum | solution.py:175
  121.9 189.6 %reduce-scatter.2.cloned.1.call-start = ((), (), s32[]{:S(2)}) async-start(), calls=%async_computation.4 | async-start | bytes 5242880 | tf_op jit(solution)/shard_map/reduce_scatter | solution.py:180
  206.4 56.0 %copy-start.1 = (bf16[64,8,2,1024]{3,1,2,0:T(8,128)(2,1)S(1)}, bf16[64,8,2,1024]{3,1,2,0:T(8,128)(2,1)}, u32[]{:S(2)}) copy-start(bf16[64,8,2,1024]{3,1,2,0:T(8,128)(2,1)} %copy.12) | copy-start | bytes 6291460
  266.7 1.2 copy-start.2
  266.7 81.3 %all-gather.8.cloned.1.call-start = ((), (), s32[]{:S(2)}) async-start(), calls=%async_computation.5 | async-start | bytes 5242880 | tf_op jit(solution)/shard_map/all_gather | solution.py:189
  268.3 26.5 %collective-permute-start = (bf16[256,2048]{1,0:T(8,128)(2,1)S(1)}, bf16[256,2048]{1,0:T(8,128)(2,1)S(1)}, u32[]{:S(2)}, u32[]{:S(2)}) collective-permute-start(bf16[256,2048]{1,0:T(8,128)(2,1)S(1)} %reshape.23), channel_id=1, source_target_pairs={{4,0},{8,4},{12,8},{16,12},{20,16},{24,20},{28,24},{5,1},{9,5},{13... | collective-permute-start | bytes 3145736 | tf_op jit(solution)/shard_map/ppermute | solution.py:18
  294.7 1.0 copy-start.3
Sparse Core Ops, SparseCore 0:
  9.5 37.1 all-gather.3
  49.6 61.6 all-gather.5
  122.1 84.2 all-reduce.1
  266.8 44.6 reduce-scatter.1
  313.5 34.4 all-gather.7

commit v2 on v1

--- a/solution.py
+++ b/solution.py
@@ -12,10 +12,135 @@
 SUB = 8
 
 
-def from_behind(block, axis, distance):
-    devices = range(lax.axis_size(axis))
-    route = [(i - distance, i) for i in devices if i - distance in devices]
-    return lax.ppermute(block, axis, route)
+MESH = pl.DeviceIdType.MESH
+CHUNKS = 8
+
+
+def partner(me, distance):
+    span = 2 * distance
+    return lax.div(me, span) * span + lax.rem(lax.rem(me, span) + distance, span)
+
+
+def distances(n):
+    found = []
+    while n > 1:
+        n //= 2
+        found.append(n)
+    return found
+
+
+def gather_kernel(axis, n, last, block_ref, out_ref, send_sem, recv_sem):
+    shifted = last is not None
+    me = lax.axis_index(axis)
+    rows = block_ref.shape[0]
+    piece = rows // CHUNKS
+    steps = distances(n)
+
+    barrier = pltpu.get_barrier_semaphore()
+    for s in steps:
+        pl.semaphore_signal(barrier, inc=1, device_id={axis: partner(me, s)}, device_id_type=MESH)
+    if shifted:
+        bond = lax.axis_index("bond")
+        for way in (1, last):
+            to = lax.rem(bond + way, last + 1)
+            pl.semaphore_signal(barrier, inc=1, device_id={"bond": to}, device_id_type=MESH)
+    pl.semaphore_wait(barrier, len(steps) + (2 if shifted else 0))
+
+    def owner(mask):
+        at = me
+        for s in steps:
+            if mask & s:
+                at = partner(at, s)
+        return at
+
+    def slot(mask, k):
+        start = pl.multiple_of(owner(mask) * rows + k * piece, piece)
+        return out_ref.at[pl.ds(start, piece), :]
+
+    def own(k):
+        return block_ref.at[k * piece:(k + 1) * piece, :]
+
+    def copy(mask, s, k):
+        source = slot(mask, k) if mask or shifted else own(k)
+        return pltpu.make_async_remote_copy(
+            src_ref=source,
+            dst_ref=slot(mask, k),
+            send_sem=send_sem.at[mask + s, k],
+            recv_sem=recv_sem.at[mask + s, k],
+            device_id={axis: partner(me, s)},
+            device_id_type=MESH,
+        )
+
+    def behind(k):
+        return pltpu.make_async_remote_copy(
+            src_ref=own(k),
+            dst_ref=slot(0, k),
+            send_sem=send_sem.at[0, k],
+            recv_sem=recv_sem.at[0, k],
+            device_id={"bond": bond - 1},
+            device_id_type=MESH,
+        )
+
+    def lower_steps(mask):
+        return [s for s in steps if mask == 0 or s < (mask & -mask)]
+
+    order = [m for s in steps for m in range(s, n, 2 * s)]
+
+    def spread():
+        for s in steps:
+            for k in range(CHUNKS):
+                if shifted and s == steps[0]:
+                    behind(k).wait_recv()
+                copy(0, s, k).start()
+        for mask in order:
+            for k in range(CHUNKS):
+                copy(mask - (mask & -mask), mask & -mask, k).wait_recv()
+                for s in lower_steps(mask):
+                    copy(mask, s, k).start()
+        for mask in [0] + order:
+            for s in lower_steps(mask):
+                for k in range(CHUNKS):
+                    copy(mask, s, k).wait_send()
+
+    if not shifted:
+        start = pl.multiple_of(me * rows, rows)
+        spread()
+        out_ref[pl.ds(start, rows), :] = block_ref[...]
+        return
+
+    @pl.when(bond > 0)
+    def _():
+        for k in range(CHUNKS):
+            behind(k).start()
+
+    @pl.when(bond < last)
+    def _():
+        spread()
+
+    @pl.when(bond == last)
+    def _():
+        out_ref[...] = jnp.zeros_like(out_ref)
+
+    @pl.when(bond > 0)
+    def _():
+        for k in range(CHUNKS):
+            behind(k).wait_send()
+
+
+def gather(block, axis, n, last, number):
+    rows, columns = block.shape
+    return pl.pallas_call(
+        functools.partial(gather_kernel, axis, n, last),
+        out_shape=jax.ShapeDtypeStruct((n * rows, columns), block.dtype),
+        in_specs=[pl.BlockSpec(memory_space=pltpu.VMEM)],
+        out_specs=pl.BlockSpec(memory_space=pltpu.VMEM),
+        scratch_shapes=[pltpu.SemaphoreType.DMA((n, CHUNKS)), pltpu.SemaphoreType.DMA((n, CHUNKS))],
+        compiler_params=pltpu.CompilerParams(
+            collective_id=number, has_side_effects=True, vmem_limit_bytes=16 * 1024 * 1024
+        ),
+        cost_estimate=pl.CostEstimate(flops=0, bytes_accessed=100 * 1024 * 1024, transcendentals=0),
+        name="gather",
+    )(block)
 
 
 def split(x):
@@ -66,7 +191,67 @@
     return jnp.concatenate(rows, axis=0)
 
 
-def solve_kernel(scale, gram_ref, sketch_ref, flat_ref, tall_ref, work, wide):
+def add_up(n, gram_ref, work, near, far, sums, others, send_sem, recv_sem):
+    size = gram_ref.shape[0]
+    blocks, half = size // LANES, LANES // 2
+    me = lax.axis_index("row")
+    steps = distances(n)[::-1]
+    mine = lax.rem(me, 2)
+
+    barrier = pltpu.get_barrier_semaphore()
+    for s in steps:
+        pl.semaphore_signal(barrier, inc=1, device_id={"row": partner(me, s)}, device_id_type=MESH)
+    pl.semaphore_wait(barrier, len(steps))
+
+    def rows(i, side):
+        return pl.ds(pl.multiple_of(i * LANES + side * half, half), half)
+
+    def copy(source, target, stage, s, i):
+        return pltpu.make_async_remote_copy(
+            src_ref=source,
+            dst_ref=target,
+            send_sem=send_sem.at[stage, i],
+            recv_sem=recv_sem.at[stage, i],
+            device_id={"row": partner(me, s)},
+            device_id_type=MESH,
+        )
+
+    def packed(ref, i):
+        return ref.at[i * half:(i + 1) * half, i * LANES:]
+
+    def first(i):
+        return copy(gram_ref.at[rows(i, 1 - mine), i * LANES:], packed(near, i), 0, 1, i)
+
+    def across(j, i):
+        return copy(packed(sums, i), packed(far.at[j], i), j + 1, steps[j + 1], i)
+
+    def back(i):
+        return copy(packed(sums, i), packed(others, i), len(steps), 1, i)
+
+    for i in range(blocks):
+        first(i).start()
+    for i in range(blocks):
+        first(i).wait()
+        packed(sums, i)[...] = gram_ref[rows(i, mine), i * LANES:] + packed(near, i)[...]
+        if len(steps) > 1:
+            across(0, i).start()
+        else:
+            back(i).start()
+    for j in range(len(steps) - 1):
+        for i in range(blocks):
+            across(j, i).wait()
+            packed(sums, i)[...] = packed(sums, i)[...] + packed(far.at[j], i)[...]
+            if j + 2 < len(steps):
+                across(j + 1, i).start()
+            else:
+                back(i).start()
+    for i in range(blocks):
+        back(i).wait()
+        work[rows(i, mine), i * LANES:size] = packed(sums, i)[...]
+        work[rows(i, 1 - mine), i * LANES:size] = packed(others, i)[...]
+
+
+def solve_kernel(scale, n, gram_ref, sketch_ref, flat_ref, tall_ref, work, wide, *exchange):
     size = gram_ref.shape[0]
     blocks = size // LANES
     width = size + sketch_ref.shape[1]
@@ -75,15 +260,18 @@
         == lax.broadcasted_iota(jnp.int32, (LANES, LANES), 1)
     )
 
+    for d in range(1, blocks):
+        work[d * LANES:(d + 1) * LANES, :d * LANES] = jnp.zeros((LANES, d * LANES), jnp.float32)
+    work[:, size:] = sketch_ref[...]
+    add_up(n, gram_ref, work, *exchange)
     total = jnp.zeros((LANES, LANES), jnp.float32)
     for d in range(blocks):
         at = slice(d * LANES, (d + 1) * LANES)
-        total = total + jnp.where(eye, gram_ref[at, at], 0.0)
+        total = total + jnp.where(eye, work[at, at], 0.0)
     ridge = jnp.sum(total, keepdims=True) * (scale * 0.01 / size)
     for d in range(blocks):
         at = slice(d * LANES, (d + 1) * LANES)
-        work[at, :size] = gram_ref[at, :] * scale
-        work[at, size:] = sketch_ref[at, :]
+        work[at, d * LANES:size] = work[at, d * LANES:size] * scale
         work[at, at] = work[at, at] + jnp.where(eye, ridge, 0.0)
 
     def eliminate(d, carry):
@@ -121,10 +309,12 @@
     lax.fori_loop(0, blocks, eliminate, 0)
 
 
-def solve(gram, sketch_t, scale):
+def solve(gram, sketch_t, scale, n, number):
     size, rows = sketch_t.shape
+    stages = len(distances(n)) + 1
+    packed = (size // 2, size)
     return pl.pallas_call(
-        functools.partial(solve_kernel, scale),
+        functools.partial(solve_kernel, scale, n),
         out_shape=(
             jax.ShapeDtypeStruct((size, rows), jnp.bfloat16),
             jax.ShapeDtypeStruct((rows, size), jnp.bfloat16),
@@ -134,8 +324,16 @@
         scratch_shapes=[
             pltpu.VMEM((size, size + rows), jnp.float32),
             pltpu.VMEM((3 * LANES, size + rows), jnp.bfloat16),
+            pltpu.VMEM(packed, jnp.float32),
+            pltpu.VMEM((max(stages - 2, 1),) + packed, jnp.float32),
+            pltpu.VMEM(packed, jnp.float32),
+            pltpu.VMEM(packed, jnp.float32),
+            pltpu.SemaphoreType.DMA((stages, size // LANES)),
+            pltpu.SemaphoreType.DMA((stages, size // LANES)),
         ],
-        compiler_params=pltpu.CompilerParams(vmem_limit_bytes=48 * 1024 * 1024),
+        compiler_params=pltpu.CompilerParams(
+            collective_id=number, has_side_effects=True, vmem_limit_bytes=48 * 1024 * 1024
+        ),
         cost_estimate=pl.CostEstimate(
             flops=4 * size * size * (size + rows), bytes_accessed=4 * size * (size + 2 * rows), transcendentals=size
         ),
@@ -147,9 +345,10 @@
     row_count = left_site.shape[0]
     bond_width = left_site.shape[1]
     kept_rank = omega.shape[1]
+    group = lax.axis_size("row")
     product = jnp.dot(
         left_site,
-        lax.all_gather(right_site, "row", axis=0, tiled=True),
+        gather(right_site, "row", group, None, 0),
         preferred_element_type=jnp.float32,
     )
     mixed = jnp.einsum(
@@ -172,21 +371,19 @@
         over,
         preferred_element_type=jnp.float32,
     )
-    gram = lax.psum(local_gram, "row")
-    left_t, left_new = solve(gram, sketch_t, 1.0 / (2.0 * bond_width))
+    left_t, left_new = solve(local_gram, sketch_t, 1.0 / (2.0 * bond_width), group, 1)
     right_scale = 1.0 / math.sqrt(2.0 * bond_width)
-    own_rows = kept_rank // lax.axis_size("row")
-    following = from_behind(left_new.reshape(row_count // 2, 2 * kept_rank), "bond", -1)
-    right_new = lax.psum_scatter(
-        (jnp.dot(left_t, theta, preferred_element_type=jnp.float32) * right_scale).astype(jnp.bfloat16),
-        "row",
-        scatter_dimension=0,
-        tiled=True,
+    own_rows = kept_rank // group
+    partial = (jnp.dot(left_t, theta, preferred_element_type=jnp.float32) * right_scale).astype(jnp.bfloat16)
+    partial, ahead = lax.optimization_barrier((partial, left_new))
+    right_new = lax.psum_scatter(partial, "row", scatter_dimension=0, tiled=True)
+    following = gather(
+        ahead.reshape(row_count // 2, 2 * kept_rank), "row", group, lax.axis_size("bond") - 1, 2
     )
     right_view = right_new.reshape(2 * own_rows, bond_width)
     pair_sum = jnp.dot(
         right_view,
-        lax.all_gather(following, "row", axis=0, tiled=True),
+        following,
         preferred_element_type=jnp.float32,
     )
     odd_pair = (pair_sum * (1.0 / math.sqrt(1.0 * bond_width))).astype(jnp.bfloat16)

time: 361 us -> 248 us (0.69)
  waiting for transfers between devices: 249 us -> 33.9 us
  Pallas kernels: 56 us -> 162 us
    pallas_call x1 -> x3, Pallas kernels: 56 us -> 162 us  [the longest x1 86.3 us: solve(): pl.pallas_call(functools.partial(solve_kernel, scale, n), out_shape=(jax....]
    psum x1 -> x0, waiting for transfers between devices: 84.2 us -> none  [shards(): gram = lax.psum(local_gram, 'row')]
    all_gather x2 -> x0, waiting for transfers between devices: 72.3 us -> none  [the longest x1 37.3 us: shards(): lax.all_gather(right_site, 'row', axis=0, tiled=True)]
    ppermute x1 -> x0, waiting for transfers between devices: 25.2 us -> none  [from_behind(): return lax.ppermute(block, axis, route)]
    all_gather x1, waiting for transfers between devices: 49.7 us -> 25.9 us  [shards(): lax.all_gather(omega, ('bond', 'row'), axis=0, tiled=True)]
    reduce_scatter x1, waiting for transfers between devices: 15.8 us -> 7.29 us  [shards(): lax.psum_scatter(partial, 'row', scatter_dimension=0, tiled=True)]
  transfers between devices with their start and end apart: 6 -> 2, of which waited for: 6 -> 2; matrix products, arithmetic and copies ran while one was open for 5% -> 5% of each run, Pallas kernels for 0% -> 31%
where the time goes in v2:
time: 248 us; the launch traced here: 247 us
  Pallas kernels  162 us (65%)
  waiting for transfers between devices  33.9 us (14%)
  matrix products  27.4 us (11%)
  between operations  14.2 us (6%)
  local copies, waits for them, and re-layouts  9.97 us (4%)
    pallas_call x1, Pallas kernels, solve(): pl.pallas_call(functools.partial(solve_kernel, scale, n), out_shape=(jax....  86.3 us
    pallas_call x2, Pallas kernels, gather(): pl.pallas_call(functools.partial(gather_kernel, axis, n, last), out_shape...  75.5 us
    all_gather x1, waiting for transfers between devices, shards(): lax.all_gather(omega, ('bond', 'row'), axis=0, tiled=True)  25.9 us
    reduce_scatter x1, waiting for transfers between devices, shards(): lax.psum_scatter(partial, 'row', scatter_dimension=0, tiled=True)  7.29 us
    dot_general x1, matrix products, shards(): jnp.dot(right_view, following, preferred_element_type=jnp.float32)  5.85 us
    dot_general x1, matrix products, shards(): lax.dot_general(jnp.concatenate([high, high, low], axis=1), jnp.concatena...  5.4 us
  transfers between devices with their start and end apart: 2, of which 2 were waited for; matrix products, arithmetic and copies ran while one was open for 5% of the time, Pallas kernels for 31%

profile of v2, /device:TPU:0, one launch (start us, length us, event | category | flops | bytes accessed | tf_op | source)
XLA Modules:
  0.0 247.4 jit_solution(3737240624305382497)
XLA Ops:
  7.2 0.0 copy-start
  7.2 0.0 all-gather.2.cloned.1.call-start
  7.2 0.7 all-gather.2.cloned.1.call-update
  7.9 0.0 reduce-scatter.2.cloned.1.call-start
  8.0 1.2 copy-done.2
  9.2 29.4 %gather.2 = bf16[1024,2048]{1,0:T(8,128)(2,1)S(1)} custom-call(bf16[256,2048]{1,0:T(8,128)(2,1)S(1)} %copy-done.2), custom_call_target="tpu_custom_call" | custom-call | bytes 104857600 | tf_op jit(solution)/shard_map/gather/pallas_call | solution.py:132
  38.6 3.7 %fusion.16 = bf16[512,2048]{1,0:T(8,128)(2,1)} fusion(bf16[512,1024]{1,0:T(8,128)(2,1)S(1)} %copy-done, bf16[1024,2048]{1,0:T(8,128)(2,1)S(1)} %gather.2), kind=kOutput, calls=%fused_computation.19 | convolution fusion | flops 2147483648 | bytes 7340032 | tf_op jit(solution)/shard_map/dot_general | solution.py:349
  42.3 3.3 %reshape.24 = bf16[256,2,2,1024,1]{3,2,1,0,4:T(2,128)(2,1)S(1)} reshape(bf16[512,2048]{1,0:T(8,128)(2,1)} %fusion.16) | data formatting | bytes 4194304 | tf_op jit(solution)/shard_map/reshape | solution.py:357
  45.6 0.1 reshape.21
  45.7 3.6 %bitcast_convert_fusion = bf16[256,1024,2,2]{1,3,2,0:T(2,128)(2,1)S(1)} fusion(bf16[256,2,2,1024,1]{3,2,1,0,4:T(2,128)(2,1)S(1)} %reshape.24, bf16[2,2,2,2]{3,2,1,0:T(2,128)(2,1)S(1)} %reshape.21), kind=kOutput, calls=%fused_computation.1 | convolution fusion | flops 8388608 | bytes 4194336 | tf_op jit(solution)/shard_map/stuv,auvc->astc/dot_general | solution.py:354
  49.3 0.6 copy.12
  49.9 25.9 %all-gather.2.cloned.1.call-done = bf16[2048,1024]{1,0:T(8,128)(2,1)} async-done(((bf16[64,1024]{1,0:T(8,128)(2,1)}), bf16[2048,1024]{1,0:T(8,128)(2,1)}) %all-gather.2.cloned.1.call-update) | async-done | bytes 4194320 | tf_op jit(solution)/shard_map/all_gather | solution.py:361
  75.9 4.6 %subtract_convert_fusion = (bf16[1024,512]{1,0:T(8,128)(2,1)S(1)}, bf16[1024,512]{1,0:T(8,128)(2,1)S(1)}, f32[1024,512]{1,0:T(8,128)S(1)}) fusion(bf16[512,2048]{1,0:T(8,128)(2,1)S(1)} %bitcast.25, bf16[2048,1024]{1,0:T(8,128)(2,1)} %all-gather.2.cloned.1.call-done), kind=kOutput, calls=%fused_computation.14 | convolution fusion | flops 2149580800 | bytes 10485760 | tf_op jit(solution)/shard_map/dot_general | solution.py:360
  80.5 5.4 %fusion.5.gram_ref = f32[1024,1024]{1,0:T(8,128)} fusion(bf16[1024,512]{1,0:T(8,128)(2,1)S(1)} %get-tuple-element.12, bf16[1024,512]{1,0:T(8,128)(2,1)S(1)} %get-tuple-element.11), kind=kOutput, calls=%fused_computation.8 | convolution fusion | flops 3240099840 | bytes 6291456 | tf_op jit(solution)/shard_map/dot_general | solution.py:368
  85.9 86.3 %solve.1 = (bf16[1024,512]{1,0:T(8,128)(2,1)S(1)}, bf16[512,1024]{1,0:T(8,128)(2,1)S(1)}) custom-call(f32[1024,1024]{1,0:T(8,128)} %fusion.5.gram_ref, f32[1024,512]{1,0:T(8,128)S(1)} %get-tuple-element.13.sketch_ref), custom_call_target="tpu_custom_call" | custom-call | flops 6442450944 | bytes 8388608 | tf_op jit(solution)/shard_map/solve/pallas_call | solution.py:316
  172.2 4.3 %multiply_convert_fusion = bf16[1024,2048]{1,0:T(8,128)(2,1)} fusion(bf16[1024,512]{1,0:T(8,128)(2,1)S(1)} %get-tuple-element.8, bf16[512,2048]{1,0:T(8,128)(2,1)S(1)} %bitcast.26), kind=kOutput, calls=%fused_computation | convolution fusion | flops 2151677952 | bytes 7340032 | tf_op jit(solution)/shard_map/dot_general | solution.py:377
  176.5 0.0 reduce-scatter.2.cloned.1.call-update
  176.5 0.4 reshape.23.block_ref
  176.9 46.1 %gather.3 = bf16[1024,2048]{1,0:T(8,128)(2,1)S(1)} custom-call(bf16[256,2048]{1,0:T(8,128)(2,1)S(1)} %reshape.23.block_ref), custom_call_target="tpu_custom_call" | custom-call | bytes 104857600 | tf_op jit(solution)/shard_map/gather/pallas_call | solution.py:132
  223.0 2.0 copy-done.1
  225.0 7.3 %reduce-scatter.2.cloned.1.call-done = bf16[256,2048]{1,0:T(8,128)(2,1)} async-done(((bf16[1024,2048]{1,0:T(8,128)(2,1)}), bf16[256,2048]{1,0:T(8,128)(2,1)}) %reduce-scatter.2.cloned.1.call-update) | async-done | bytes 1048592 | tf_op jit(solution)/shard_map/reduce_scatter | solution.py:379
  232.3 1.4 reshape.22
  233.7 5.8 %multiply_convert_fusion.1 = bf16[512,2048]{1,0:T(8,128)(2,1)} fusion(bf16[512,1024]{1,0:T(8,128)(2,1)S(1)} %reshape.22, bf16[1024,2048]{1,0:T(8,128)(2,1)} %copy-done.1), kind=kOutput, calls=%fused_computation.4 | convolution fusion | flops 2149580800 | bytes 7340032 | tf_op jit(solution)/shard_map/dot_general | solution.py:384
  239.6 1.0 copy.18
  (9 shorter events, 0.0 us)
Async XLA Ops:
  7.2 31.4 %copy-start = (bf16[512,1024]{1,0:T(8,128)(2,1)S(1)}, bf16[512,1024]{1,0:T(8,128)(2,1)}, u32[]{:S(2)}) copy-start(bf16[512,1024]{1,0:T(8,128)(2,1)} %param.4) | copy-start | bytes 3145732
  7.2 68.7 %all-gather.2.cloned.1.call-start = ((), (), s32[]{:S(2)}) async-start(), calls=%async_computation.1 | async-start | bytes 4325376 | tf_op jit(solution)/shard_map/all_gather | solution.py:361
  7.9 224.4 %reduce-scatter.2.cloned.1.call-start = ((), (), s32[]{:S(2)}) async-start(), calls=%async_computation.2 | async-start | bytes 5242880 | tf_op jit(solution)/shard_map/reduce_scatter | solution.py:379
  8.0 1.2 copy-start.2
  42.3 3.3 %copy-start.5 = (f32[4,4]{1,0:T(4,128)S(1)}, f32[4,4]{1,0:T(4,128)}, u32[]{:S(2)}) copy-start(f32[4,4]{1,0:T(4,128)} %param.6) | copy-start | bytes 196
  49.9 30.5 %copy-start.3 = (bf16[64,8,2,1024]{3,1,2,0:T(8,128)(2,1)}, bf16[64,8,2,1024]{3,1,2,0:T(8,128)(2,1)S(1)}, u32[]{:S(2)}) copy-start(bf16[64,8,2,1024]{3,1,2,0:T(8,128)(2,1)S(1)} %copy.12) | copy-start | bytes 6291460
  85.9 86.3 %copy-start.4 = (bf16[64,8,2,1024]{3,1,2,0:T(8,128)(2,1)S(1)}, bf16[64,8,2,1024]{3,1,2,0:T(8,128)(2,1)}, u32[]{:S(2)}) copy-start(bf16[64,8,2,1024]{3,1,2,0:T(8,128)(2,1)} %copy-done.3) | copy-start | bytes 6291460
  223.0 2.0 copy-start.1
Sparse Core Ops, SparseCore 0:
  10.9 64.9 all-gather.1
  176.6 55.6 reduce-scatter.1
